TPU v7x, 256 devices: a whole 4x4x8 slice. The times are simulated.
256 devices in a mesh: blk: 32 (over z, y), rep: 8 (over x, core).
Axes of the slice: x: 4, y: 4, z: 8, core: 2. Of those that a mesh axis runs over, the one named last changes fastest.
Arguments:
- tensor_blocks: bfloat16 [512, 128, 128, 128], P(('blk', 'rep')), may hold values from -15 to 15
- triples: int32 [512, 3], P(('blk', 'rep')), may hold values from 0 to 63, as said below
- slot_count: int32 [256], P(('blk', 'rep')), may hold values from 1 to 2, as said below
- factor: bfloat16 [8192, 256], P('blk', 'rep'), may hold values from -0.19743253 to 0.19743253
Outputs:
- gradient: float32 [8192, 256], P('blk', 'rep')
Inputs may be any that keep to these rules, and one draw needn't show every extreme that they name: `triples`: each row is i >= j >= k; equal indices occur; the different row blocks named by the 2 slots of one device have different values of block // 2. `slot_count`: the first device's entry is 2.
All inputs are finite; a program needn't handle non-finite values.
Results may differ from a plain program's by a relative error of at most 0.003.
Values may be sent and summed in bfloat16 or wider, within the bound.
No kernel may reach another device: no remote copies, remote signals or barrier semaphores. Data moves between devices by JAX's collectives and lax.ppermute only.
A program may use at most 128 MiB of HBM per device.

v0:
```python
import jax
import jax.numpy as jnp
from jax import lax
from jax.sharding import Mesh
from jax.sharding import PartitionSpec as P

BLK = ("blk_0", "blk_1")
BLK_REP = ("blk_0", "blk_1", "rep")


def copy_for_each(array, axis):
    peers = lax.axis_size(axis)
    return lax.all_to_all(
        jnp.broadcast_to(array[None], (peers, *array.shape)), axis, 0, 0, tiled=True
    )


def joined_along(tiles, dim):
    shape = list(tiles.shape[1:])
    shape[dim] *= tiles.shape[0]
    return jnp.moveaxis(tiles, 0, dim).reshape(shape)


def collect(array, axis, dim):
    tiles = copy_for_each(array, axis)
    return joined_along(tiles, dim)


def gathered_by_axis(array, axes, dim):
    whole = array
    for number in range(len(axes) - 1, -1, -1):
        whole = lax.all_gather(whole, axes[number], axis=dim, tiled=True)
    return whole


def split_up(array, dim, peers):
    shape = array.shape
    tiles = array.reshape(*shape[:dim], peers, shape[dim] // peers, *shape[dim + 1 :])
    return jnp.moveaxis(tiles, dim, 0)


def sent_and_summed(array, axis, dim):
    tiles = split_up(array, dim, lax.axis_size(axis))
    arrived = lax.all_to_all(tiles, axis, split_axis=0, concat_axis=0, tiled=True)
    return arrived.sum(axis=0)


def side_weights(triples):
    first_idx = triples[:, 0]
    second_idx = triples[:, 1]
    third_idx = triples[:, 2]
    same_upper = first_idx == second_idx
    same_lower = second_idx == third_idx
    apart = jnp.logical_and(jnp.logical_not(same_upper), jnp.logical_not(same_lower))
    every = jnp.logical_and(same_upper, same_lower)
    base = jnp.where(apart, 2.0, 1.0).astype(jnp.float32)
    dropped = jnp.where(every, 0.0, base)
    return jnp.stack([base, dropped, dropped], axis=1)


def contract(block, upper, middle, lower):
    edge_size = block.shape[0]
    rank_width = upper.shape[1]
    by_lower = jnp.dot(
        block.reshape(edge_size * edge_size, edge_size), lower, preferred_element_type=jnp.float32
    ).reshape(edge_size, edge_size, rank_width)
    by_upper = lax.dot_general(
        block.reshape(edge_size, edge_size * edge_size),
        upper,
        (((0,), (0,)), ((), ())),
        preferred_element_type=jnp.float32,
    ).reshape(edge_size, edge_size, rank_width)
    upper_wide = upper.astype(jnp.float32)
    middle_wide = middle.astype(jnp.float32)
    to_first = jnp.einsum("abr,br->ar", by_lower, middle_wide, precision=lax.Precision.HIGHEST)
    to_second = jnp.einsum("abr,ar->br", by_lower, upper_wide, precision=lax.Precision.HIGHEST)
    to_third = jnp.einsum("bcr,br->cr", by_upper, middle_wide, precision=lax.Precision.HIGHEST)
    return (to_first, to_second, to_third)


def shards(tensor_blocks, triples, slot_count, factor):
    own_rows = collect(factor, "rep", 1)
    block_size = tensor_blocks.shape[1]
    rank_width = own_rows.shape[1]
    owner_count = lax.axis_size(BLK)
    per_owner = own_rows.shape[0] // block_size
    block_count = owner_count * per_owner
    gathered = gathered_by_axis(own_rows, BLK, 0)
    table = gathered.reshape(block_count, block_size, rank_width)
    divisor = 1
    gram_matrix = lax.dot_general(
        gathered, gathered, (((0,), (0,)), ((), ())), preferred_element_type=jnp.float32
    )
    slot_total = tensor_blocks.shape[0]
    alive = (jnp.arange(slot_total, dtype=jnp.int32) < slot_count[0]).astype(jnp.float32)
    weights = side_weights(triples) * alive[:, None]
    results = []
    for slot_index in range(slot_total):
        triple = triples[slot_index]
        upper = table[triple[0] // divisor]
        middle = table[triple[1] // divisor]
        lower = table[triple[2] // divisor]
        results.extend(contract(tensor_blocks[slot_index], upper, middle, lower))
    stacked = jnp.stack(results, axis=0)
    targets = triples.reshape(-1)
    flat_weights = weights.reshape(-1)
    hadamard = gram_matrix * gram_matrix
    column_width = factor.shape[1]
    column_start = lax.axis_index("rep") * column_width
    hadamard_cols = lax.dynamic_slice_in_dim(hadamard, column_start, column_width, 1)
    fitted = jnp.dot(
        own_rows.astype(jnp.float32),
        hadamard_cols,
        preferred_element_type=jnp.float32,
        precision=lax.Precision.HIGHEST,
    )
    owner_table = (jnp.arange(block_count, dtype=jnp.int32)[:, None] == targets[None, :]).astype(
        jnp.float32
    )
    owner_table = owner_table * flat_weights[None, :]
    partial_value = jnp.einsum(
        "bs,sar->bar", owner_table, stacked, precision=lax.Precision.HIGHEST
    ).reshape(block_count * block_size, rank_width)
    halfway = lax.psum_scatter(partial_value, "rep", scatter_dimension=1, tiled=True)
    owned_sum = sent_and_summed(halfway, BLK, 0)
    return fitted - owned_sum


def solution(mesh):
    split = Mesh(mesh.devices.reshape(8, 4, mesh.shape["rep"]), ("blk_0", "blk_1", "rep"))
    in_specs = (P(BLK_REP, None, None, None), P(BLK_REP, None), P(BLK_REP), P(BLK, "rep"))
    out_specs = P(BLK, "rep")
    return jax.shard_map(
        shards, mesh=split, in_specs=in_specs, out_specs=out_specs, check_vma=False
    )
```

profile of v0, /device:TPU:8, one launch (start us, length us, event | category | flops | bytes accessed | tf_op | source)
XLA Modules:
  0.0 325.7 jit_solution(6249507429740337569)
XLA Ops:
  6.5 0.0 all-gather.2.cloned.1.call-start
  6.5 0.7 broadcast_in_dim.20
  7.3 10.2 %all_to_all.10 = bf16[8,256,32]{1,2,0:T(8,128)(2,1)S(1)} all-to-all(bf16[8,256,32]{1,2,0:T(8,128)(2,1)S(1)} %broadcast_in_dim.20), channel_id=1, replica_groups=mesh['blk_0'=8,'blk_1'=4,'rep'=8] {'rep'}, dimensions={0} | all-to-all | bytes 262144 | tf_op jit(solution)/shard_map/all_to_all | solution.py:13
  17.5 14.4 %all_gather.6 = bf16[1024,256]{0,1:T(8,128)(2,1)} all-gather(bf16[256,256]{0,1:T(8,128)(2,1)S(1)} %bitcast.131), channel_id=1, replica_groups=mesh['blk_0'=8,'blk_1'=4,'rep'=8] {'blk_1'}, dimensions={0}, use_global_device_ids=true | all-gather | bytes 655360 | tf_op jit(solution)/shard_map/all_gather | solution.py:32
  31.8 0.0 all-gather.2.cloned.1.call-update
  31.9 0.0 reduce-scatter.4.cloned.1.call-start
  31.9 0.8 eq.26
  32.7 1.6 fusion.26
  42.5 0.9 and_select_fusion.1
  43.4 0.1 maximum_multiply_fusion
  43.4 0.1 mul.33
  47.3 6.1 %fusion.25 = (bf16[1,128,128,128]{3,2,1,0:T(8,128)(2,1)}, bf16[1,128,128,128]{3,2,1,0:T(8,128)(2,1)}) fusion(bf16[2,128,128,128]{3,2,1,0:T(8,128)(2,1)} %param.4), kind=kLoop, calls=%fused_computation.48 | loop fusion | bytes 16777216 | tf_op jit(solution)/shard_map/slice | solution.py:103
  53.4 34.0 %all-gather.2.cloned.1.call-done = bf16[8192,256]{0,1:T(8,128)(2,1)} async-done(((bf16[1024,256]{0,1:T(8,128)(2,1)}), bf16[8192,256]{0,1:T(8,128)(2,1)}) %all-gather.2.cloned.1.call-update) | async-done | bytes 4194320 | tf_op jit(solution)/shard_map/all_gather | solution.py:32
  87.4 6.4 %copy.62 = bf16[8192,256]{1,0:T(8,128)(2,1)} copy(bf16[8192,256]{0,1:T(8,128)(2,1)} %all-gather.2.cloned.1.call-done) | data formatting | bytes 8388608 | tf_op jit(solution)/shard_map/reshape | solution.py:89
  93.7 1.0 bitcast_convert_fusion
  94.7 0.1 copy.68
  94.8 0.1 copy.67
  94.9 0.1 copy.64
  95.0 0.1 copy.65
  95.1 4.6 %convolution_bitcast_fusion.3 = f32[32,8,128,128]{3,1,2,0:T(8,128)S(1)} fusion(bf16[16384,128]{1,0:T(8,128)(2,1)} %bitcast.121, bf16[64,128,256]{2,1,0:T(8,128)(2,1)} %bitcast.127, s32[]{:T(128)S(6)} %select_n.44), kind=kOutput, calls=%fused_computation.9 | convolution fusion | flops 1073741824 | bytes 21037060 | tf_op jit(solution)/shard_map/dot_general | solution.py:64
  99.7 3.8 %copy.70 = f32[32,8,128,128]{3,2,1,0:T(8,128)S(1)} copy(f32[32,8,128,128]{3,1,2,0:T(8,128)S(1)} %convolution_bitcast_fusion.3) | data formatting | bytes 33554432
  103.5 0.0 copy-start
  103.6 5.7 %copy-done = f32[32,8,128,128]{3,2,1,0:T(8,128)} copy-done((f32[32,8,128,128]{3,2,1,0:T(8,128)}, f32[32,8,128,128]{3,2,1,0:T(8,128)S(1)}, u32[]{:S(2)}) %copy-start) | copy-done | bytes 16777240
  109.3 6.1 %multiply_reduce_fusion.4 = f32[256,128]{1,0:T(8,128)S(1)} fusion(f32[256,128]{1,0:T(8,128)S(1)} %copy.65, f32[32,8,128,128]{3,2,1,0:T(8,128)S(1)} %copy.70), kind=kLoop, calls=%fused_computation.4 | loop fusion | flops 8355840 | bytes 17039360
  115.4 0.1 copy.35
  115.5 0.1 stack.29
  115.6 8.2 %multiply_reduce_fusion.5 = f32[256,128]{1,0:T(8,128)S(1)} fusion(f32[128,128,256]{1,0,2:T(8,128)} %bitcast.117, f32[256,128]{1,0:T(8,128)S(1)} %copy.64), kind=kLoop, calls=%fused_computation.5 | loop fusion | flops 8355840 | bytes 17039360
  123.8 0.1 copy.29
  123.9 0.1 stack.28
  124.0 5.8 %convolution_bitcast_fusion.2 = f32[32,8,128,128]{3,1,2,0:T(8,128)S(1)} fusion(bf16[16,8,128,128]{3,2,1,0:T(8,128)(2,1)} %bitcast.122, bf16[64,128,256]{2,1,0:T(8,128)(2,1)} %bitcast.128, s32[]{:T(128)S(6)} %select_n.45), kind=kOutput, calls=%fused_computation.8 | convolution fusion | flops 1073741824 | bytes 21037060 | tf_op jit(solution)/shard_map/dot_general | solution.py:67
  129.8 6.7 %copy.72 = f32[32,8,128,128]{3,2,1,0:T(8,128)} copy(f32[32,8,128,128]{3,1,2,0:T(8,128)S(1)} %convolution_bitcast_fusion.2) | data formatting | bytes 33554432
  136.5 7.6 %multiply_reduce_fusion.3 = f32[256,128]{1,0:T(8,128)S(1)} fusion(f32[256,128]{1,0:T(8,128)S(1)} %copy.64, f32[32,8,128,128]{3,2,1,0:T(8,128)} %copy.72), kind=kLoop, calls=%fused_computation.3 | loop fusion | flops 8355840 | bytes 17039360
  144.1 0.1 copy.41
  144.2 0.1 stack.30
  144.3 4.6 %convolution_bitcast_fusion.1 = f32[32,8,128,128]{3,1,2,0:T(8,128)S(1)} fusion(bf16[16384,128]{1,0:T(8,128)(2,1)} %bitcast.119, bf16[64,128,256]{2,1,0:T(8,128)(2,1)} %bitcast.129, s32[]{:T(128)S(6)} %select_n.47), kind=kOutput, calls=%fused_computation.7 | convolution fusion | flops 1073741824 | bytes 21037060 | tf_op jit(solution)/shard_map/dot_general | solution.py:64
  148.9 4.0 %copy.73 = f32[32,8,128,128]{3,2,1,0:T(8,128)S(1)} copy(f32[32,8,128,128]{3,1,2,0:T(8,128)S(1)} %convolution_bitcast_fusion.1) | data formatting | bytes 33554432
  152.9 0.0 copy-start.1
  152.9 5.7 %copy-done.1 = f32[32,8,128,128]{3,2,1,0:T(8,128)} copy-done((f32[32,8,128,128]{3,2,1,0:T(8,128)}, f32[32,8,128,128]{3,2,1,0:T(8,128)S(1)}, u32[]{:S(2)}) %copy-start.1) | copy-done | bytes 16777240
  158.6 6.1 %multiply_reduce_fusion.1 = f32[256,128]{1,0:T(8,128)S(1)} fusion(f32[256,128]{1,0:T(8,128)S(1)} %copy.68, f32[32,8,128,128]{3,2,1,0:T(8,128)S(1)} %copy.73), kind=kLoop, calls=%fused_computation.1 | loop fusion | flops 8355840 | bytes 17039360
  164.7 0.1 copy.53
  164.9 0.1 stack.32
  165.0 8.2 %multiply_reduce_fusion.2 = f32[256,128]{1,0:T(8,128)S(1)} fusion(f32[128,128,256]{1,0,2:T(8,128)} %bitcast.118, f32[256,128]{1,0:T(8,128)S(1)} %copy.67), kind=kLoop, calls=%fused_computation.2 | loop fusion | flops 8355840 | bytes 17039360
  173.2 0.1 copy.47
  173.3 0.1 stack.31
  173.4 5.8 %convolution_bitcast_fusion = f32[32,8,128,128]{3,1,2,0:T(8,128)S(1)} fusion(bf16[16,8,128,128]{3,2,1,0:T(8,128)(2,1)} %bitcast.120, bf16[64,128,256]{2,1,0:T(8,128)(2,1)} %bitcast.130, s32[]{:T(128)S(6)} %select_n.48), kind=kOutput, calls=%fused_computation.6 | convolution fusion | flops 1073741824 | bytes 21037060 | tf_op jit(solution)/shard_map/dot_general | solution.py:67
  179.2 6.7 %copy.75 = f32[32,8,128,128]{3,2,1,0:T(8,128)} copy(f32[32,8,128,128]{3,1,2,0:T(8,128)S(1)} %convolution_bitcast_fusion) | data formatting | bytes 33554432
  185.9 7.6 %multiply_reduce_fusion = f32[256,128]{1,0:T(8,128)S(1)} fusion(f32[256,128]{1,0:T(8,128)S(1)} %copy.67, f32[32,8,128,128]{3,2,1,0:T(8,128)} %copy.75), kind=kLoop, calls=%fused_computation | loop fusion | flops 8355840 | bytes 17039360
  193.5 0.1 copy.59
  193.6 0.1 stack.33
  193.7 1.5 stack.34
  195.2 6.8 %fusion.13 = f32[64,128,256]{2,0,1:T(8,128)S(1)} fusion(f32[6,128,256]{2,0,1:T(8,128)S(1)} %stack.34, f32[6]{0:T(128)S(1)} %mul.33, s32[6]{0:T(128)S(1)} %eq.26), kind=kOutput, calls=%fused_computation.29 | convolution fusion | flops 150995712 | bytes 9175088 | tf_op jit(solution)/shard_map/bs,sar->bar/dot_general | solution.py:121
  202.0 8.3 %copy.20 = f32[64,128,256]{2,1,0:T(8,128)} copy(f32[64,128,256]{2,0,1:T(8,128)S(1)} %fusion.13) | data formatting | bytes 16777216 | tf_op jit(solution)/shard_map/bs,sar->bar/dot_general | solution.py:121
  210.3 8.9 %copy.60 = f32[8192,256]{0,1:T(8,128)} copy(f32[8192,256]{1,0:T(8,128)} %bitcast.124) | data formatting | bytes 16777216
  219.3 0.0 reduce-scatter.4.cloned.1.call-update
  219.3 53.8 %reduce-scatter.4.cloned.1.call-done = f32[32,8192]{1,0:T(8,128)} async-done(((f32[256,8192]{1,0:T(8,128)}), f32[32,8192]{1,0:T(8,128)}) %reduce-scatter.4.cloned.1.call-update) | async-done | bytes 1048592
  273.1 3.6 %copy.61 = f32[8192,32]{1,0:T(8,128)} copy(f32[8192,32]{0,1:T(8,128)} %bitcast.133) | data formatting | bytes 2097152
  276.6 3.6 %copy.21 = f32[32,256,32]{1,2,0:T(8,128)} copy(f32[32,256,32]{2,1,0:T(8,128)} %bitcast.125) | data formatting | bytes 2097152 | tf_op jit(solution)/shard_map/reshape | solution.py:38
  280.3 10.2 %all-to-all-start.1 = ((f32[32,256,32]{1,2,0:T(8,128)}), f32[32,256,32]{1,2,0:T(8,128)S(1)}, u32[]{:S(2)}, u32[]{:S(2)}) async-start(f32[32,256,32]{1,2,0:T(8,128)} %copy.21), calls=%async_computation.1 | async-start | bytes 2097152 | tf_op jit(solution)/shard_map/all_to_all | solution.py:44
  290.4 4.7 %fusion.27 = f32[256,256]{0,1:T(8,128)S(1)} fusion(bf16[8192,256]{0,1:T(8,128)(2,1)} %all-gather.2.cloned.1.call-done), kind=kOutput, calls=%fused_computation.50 | convolution fusion | flops 1073741824 | bytes 4456448 | tf_op jit(solution)/shard_map/dot_general | solution.py:91
  295.2 22.8 %all-to-all-done.1 = f32[32,256,32]{1,2,0:T(8,128)S(1)} async-done(((f32[32,256,32]{1,2,0:T(8,128)}), f32[32,256,32]{1,2,0:T(8,128)S(1)}, u32[]{:S(2)}, u32[]{:S(2)}) %all-to-all-start.1) | async-done | bytes 1048608 | tf_op jit(solution)/shard_map/all_to_all | solution.py:44
  318.0 0.1 reduce_sum.9
  318.0 0.8 fusion.4
  (2 shorter events, 0.0 us)
Async XLA Ops:
  6.5 80.8 %all-gather.2.cloned.1.call-start = ((), (), s32[]{:S(2)}) async-start(), calls=%async_computation.3 | async-start | bytes 4718592 | tf_op jit(solution)/shard_map/all_gather | solution.py:32
  31.9 241.2 %reduce-scatter.4.cloned.1.call-start = ((), (), s32[]{:S(2)}) async-start(), calls=%async_computation.4 | async-start | bytes 9437184
  103.5 5.7 %copy-start = (f32[32,8,128,128]{3,2,1,0:T(8,128)}, f32[32,8,128,128]{3,2,1,0:T(8,128)S(1)}, u32[]{:S(2)}) copy-start(f32[32,8,128,128]{3,2,1,0:T(8,128)S(1)} %copy.70) | copy-start | bytes 50331652
  152.9 5.7 %copy-start.1 = (f32[32,8,128,128]{3,2,1,0:T(8,128)}, f32[32,8,128,128]{3,2,1,0:T(8,128)S(1)}, u32[]{:S(2)}) copy-start(f32[32,8,128,128]{3,2,1,0:T(8,128)S(1)} %copy.73) | copy-start | bytes 50331652
  280.3 37.7 %all-to-all-start.1 = ((f32[32,256,32]{1,2,0:T(8,128)}), f32[32,256,32]{1,2,0:T(8,128)S(1)}, u32[]{:S(2)}, u32[]{:S(2)}) async-start(f32[32,256,32]{1,2,0:T(8,128)} %copy.21), calls=%async_computation.1 | async-start | bytes 2097152 | tf_op jit(solution)/shard_map/all_to_all | solution.py:44
Sparse Core Ops, SparseCore 0:
  32.0 55.3 all-gather.1
  219.4 53.6 reduce-scatter.3
where the time goes:
time: 327 us; the launch traced here: 326 us
  waiting for transfers between devices  111 us (34%)
  local copies, waits for them, and re-layouts  75.6 us (23%)
  other arithmetic  45.8 us (14%)
  matrix products  33.3 us (10%)
  between operations  25.7 us (8%)
  blocking collectives  24.6 us (8%)
  starting transfers between devices  10.2 us (3%)
    unnamed x3, waiting for transfers between devices  53.8 us
    unnamed x14, local copies, waits for them, and re-layouts  45.5 us
    unnamed x7, other arithmetic  44.8 us
    all_gather x1, waiting for transfers between devices, gathered_by_axis(): whole = lax.all_gather(whole, axes[number], axis=dim, tiled=True)  34 us
    all_to_all x1, waiting for transfers between devices, sent_and_summed(): lax.all_to_all(tiles, axis, split_axis=0, concat_axis=0, tiled=True)  22.8 us
    all_gather x1, blocking collectives, gathered_by_axis(): whole = lax.all_gather(whole, axes[number], axis=dim, tiled=True)  14.4 us
    dot_general x2, matrix products, contract(): lax.dot_general(block.reshape(edge_size, edge_size * edge_size), upper, (...  11.7 us
    all_to_all x1, blocking collectives, copy_for_each(): lax.all_to_all(jnp.broadcast_to(array[None], (peers, *array.shape)), axis...  10.2 us
  transfers between devices with their start and end apart: 3, of which 3 were waited for; matrix products, arithmetic and copies ran while one was open for 4% of the time, Pallas kernels for 0%

commit v1 on v0

v1 whole, which is shorter than its diff:
```python
import jax
import jax.numpy as jnp
from jax import lax
from jax.experimental import pallas as pl
from jax.experimental.pallas import tpu as pltpu
from jax.sharding import Mesh
from jax.sharding import PartitionSpec as P

BLK = ("blk_0", "blk_1")
BLK_REP = ("blk_0", "blk_1", "rep")

BS = 128
CHUNK = 8
F32 = jnp.float32
BF16 = jnp.bfloat16
VMEM = pltpu.VMEM
SMEM = pltpu.SMEM


def whole(space=VMEM):
    return pl.BlockSpec(memory_space=space)


def select_kernel(names, table, own, out):
    reps, named = names.shape
    own_count = own.shape[0]
    gram_count = table.shape[0] // reps
    for peer in range(reps):
        for t in range(named):
            out[peer, t] = table[names[peer, t]]
        for t in range(own_count):
            out[peer, named + t] = own[t]
        for t in range(gram_count):
            out[peer, named + own_count + t] = table[peer * gram_count + t]


def contract_kernel(triples, count, x, sel, out, fac, lower_s, middle_s, y1, y2, y3):
    reps, tiles, width, _ = sel.shape
    rank = reps * width
    slot = pl.program_id(0)
    step = pl.program_id(1)
    steps = pl.num_programs(1)
    named = 3 * pl.num_programs(0)

    def column_major(t):
        return sel[:, t].reshape(rank, BS)

    @pl.when(step == 0)
    def _():
        for side in range(3):
            tile = sel[:, pl.ds(slot * 3 + side, 1)].reshape(rank, BS)
            fac[side] = tile.astype(F32).T
        y2[...] = jnp.zeros_like(y2)
        y3[...] = jnp.zeros_like(y3)

    @pl.when((slot == 0) & (step == 0))
    def _():
        gram = jnp.zeros((rank, rank), F32)
        for t in range(8, tiles):
            part = column_major(t)
            gram = gram + lax.dot_general(
                part, part, (((1,), (1,)), ((), ())), preferred_element_type=F32
            )
        for half in range(rank // BS):
            out[:, 6 + half] = gram[:, half * BS : (half + 1) * BS].reshape(reps, width, BS)

    blocks = x[0]
    lower = fac[2].astype(BF16)
    middle = fac[1].astype(BF16)
    lower_s[...] = jnp.dot(
        blocks.reshape(CHUNK * BS, BS), lower, preferred_element_type=F32
    ).reshape(CHUNK, BS, rank)
    turned = jnp.concatenate([blocks[a].T for a in range(CHUNK)], axis=0)
    middle_s[...] = jnp.dot(turned, middle, preferred_element_type=F32).reshape(CHUNK, BS, rank)

    row0 = pl.multiple_of(step * CHUNK, CHUNK)
    for half in range(rank // BS):
        cols = slice(half * BS, (half + 1) * BS)
        upper_rows = fac[0, pl.ds(row0, CHUNK), cols]
        spread = [jnp.broadcast_to(upper_rows[a : a + 1], (8, BS)) for a in range(CHUNK)]
        sums = [jnp.zeros((8, BS), F32) for _ in range(CHUNK)]
        for b in range(0, BS, 8):
            rows = slice(b, b + 8)
            other = fac[1, rows, cols]
            second = y2[rows, cols]
            third = y3[rows, cols]
            for a in range(CHUNK):
                value = lower_s[a, rows, cols]
                sums[a] = sums[a] + value * other
                second = second + value * spread[a]
                third = third + middle_s[a, rows, cols] * spread[a]
            y2[rows, cols] = second
            y3[rows, cols] = third
        y1[pl.ds(row0, CHUNK), cols] = jnp.concatenate(
            [jnp.sum(sums[a], axis=0, keepdims=True) for a in range(CHUNK)], axis=0
        )

    @pl.when(step == steps - 1)
    def _():
        i, j, k = triples[slot, 0], triples[slot, 1], triples[slot, 2]
        upper_tie = i == j
        lower_tie = j == k
        alive = jnp.where(slot < count[0], 1.0, 0.0)
        base = jnp.where(upper_tie | lower_tie, 1.0, 2.0) * alive
        dropped = jnp.where(upper_tie & lower_tie, 0.0, base)
        for side, (value, weight) in enumerate(((y1, base), (y2, dropped), (y3, dropped))):
            out[:, pl.ds(slot * 3 + side, 1)] = (value[...].T * weight).reshape(
                reps, 1, width, BS
            )


def scatter_kernel(names, parts, own, total, fitted):
    reps, named = names.shape
    width = parts.shape[2]
    rank = reps * width
    total[...] = jnp.zeros_like(total)
    for peer in range(reps):
        for t in range(named):
            at = names[peer, t]
            total[at] = total[at] + parts[peer, t]
    halves = []
    for half in range(rank // BS):
        gram = parts[0, named + half]
        for peer in range(1, reps):
            gram = gram + parts[peer, named + half]
        halves.append(gram)
    gram = jnp.concatenate(halves, axis=1)
    rest = gram * gram
    pieces = []
    for _ in range(3):
        piece = rest.astype(BF16)
        rest = rest - piece.astype(F32)
        pieces.append(piece)
    for t in range(fitted.shape[0]):
        rows = own[:, named + t].reshape(rank, BS)
        value = jnp.dot(pieces[2], rows, preferred_element_type=F32)
        value = value + jnp.dot(pieces[1], rows, preferred_element_type=F32)
        fitted[t] = value + jnp.dot(pieces[0], rows, preferred_element_type=F32)


def finish_kernel(arrived, fitted, out):
    for t in range(fitted.shape[0]):
        total = arrived[0, t]
        for source in range(1, arrived.shape[0]):
            total = total + arrived[source, t]
        out[t * BS : (t + 1) * BS, :] = (fitted[t] - total).T


def gathered(array, axis):
    peers = lax.axis_size(axis)
    return lax.all_to_all(
        jnp.broadcast_to(array[None], (peers, *array.shape)), axis, 0, 0, tiled=True
    )


def shards(tensor_blocks, triples, slot_count, factor):
    slots = tensor_blocks.shape[0]
    reps = lax.axis_size("rep")
    owners = lax.axis_size(BLK)
    rows, width = factor.shape
    per_owner = rows // BS
    rank = reps * width
    named = 3 * slots
    own = factor.T.reshape(width, per_owner, BS).swapaxes(0, 1)
    names = lax.all_gather(triples.reshape(1, named), "rep", axis=0, tiled=True)
    near = gathered(own, "blk_1")
    table = gathered(near, "blk_0").reshape(owners * per_owner, width, BS)
    gram_count = owners * per_owner // reps
    tiles = named + per_owner + gram_count
    chosen = pl.pallas_call(
        select_kernel,
        out_shape=jax.ShapeDtypeStruct((reps, tiles, width, BS), BF16),
        in_specs=[whole(SMEM), whole(), whole()],
        out_specs=whole(),
        name="select",
    )(names, table, own)
    chosen = lax.all_to_all(chosen, "rep", 0, 0, tiled=True)
    steps = BS // CHUNK
    parts = pl.pallas_call(
        contract_kernel,
        grid=(slots, steps),
        out_shape=jax.ShapeDtypeStruct((reps, named + rank // BS, width, BS), F32),
        in_specs=[
            whole(SMEM),
            whole(SMEM),
            pl.BlockSpec((1, CHUNK, BS, BS), lambda s, c: (s, c, 0, 0)),
            whole(),
        ],
        out_specs=whole(),
        scratch_shapes=[
            VMEM((3, BS, rank), F32),
            VMEM((CHUNK, BS, rank), F32),
            VMEM((CHUNK, BS, rank), F32),
            VMEM((BS, rank), F32),
            VMEM((BS, rank), F32),
            VMEM((BS, rank), F32),
        ],
        name="contract",
    )(triples, slot_count, tensor_blocks, chosen)
    parts = lax.all_to_all(parts, "rep", 0, 0, tiled=True)
    total, fitted = pl.pallas_call(
        scatter_kernel,
        out_shape=(
            jax.ShapeDtypeStruct((owners * per_owner, width, BS), F32),
            jax.ShapeDtypeStruct((per_owner, width, BS), F32),
        ),
        in_specs=[whole(SMEM), whole(), whole()],
        out_specs=(whole(), whole()),
        name="scatter",
    )(names, parts, chosen)
    arrived = lax.all_to_all(
        total.reshape(owners, per_owner, width, BS), BLK, 0, 0, tiled=True
    )
    return pl.pallas_call(
        finish_kernel,
        out_shape=jax.ShapeDtypeStruct((rows, width), F32),
        in_specs=[whole(), whole()],
        out_specs=whole(),
        name="finish",
    )(arrived, fitted)


def solution(mesh):
    split = Mesh(mesh.devices.reshape(8, 4, mesh.shape["rep"]), ("blk_0", "blk_1", "rep"))
    in_specs = (P(BLK_REP, None, None, None), P(BLK_REP, None), P(BLK_REP), P(BLK, "rep"))
    out_specs = P(BLK, "rep")
    return jax.shard_map(
        shards, mesh=split, in_specs=in_specs, out_specs=out_specs, check_vma=False
    )
```

time: 327 us -> 147 us (0.45)
  waiting for transfers between devices: 111 us -> 19.3 us
  local copies, waits for them, and re-layouts: 75.6 us -> 5.78 us
  blocking collectives: 24.6 us -> 74.2 us
  other arithmetic: 45.8 us -> 0 us
  matrix products: 33.3 us -> 0 us
  Pallas kernels: 0 us -> 32.9 us
  between operations: 25.7 us -> 0.67 us
    unnamed x3 -> x0, waiting for transfers between devices: 53.8 us -> none
    all_to_all x1 -> x3, blocking collectives: 10.2 us -> 62.9 us  [the longest x1 33.8 us: shards(): lax.all_to_all(total.reshape(owners, per_owner, width, BS), BLK, 0, 0, ti...]
    unnamed x7 -> x0, other arithmetic: 44.8 us -> none
    unnamed x14 -> x9, local copies, waits for them, and re-layouts: 45.5 us -> 3.25 us
    all_gather x1 -> x0, waiting for transfers between devices: 34 us -> none  [gathered_by_axis(): whole = lax.all_gather(whole, axes[number], axis=dim, tiled=True)]
    dot_general x7 -> x0, matrix products: 33.3 us -> none  [the longest x2 11.7 us: contract(): lax.dot_general(block.reshape(edge_size, edge_size * edge_size), upper, (...]
    pallas_call x0 -> x4, Pallas kernels: none -> 32.9 us  [the longest x1 26 us: shards(): pl.pallas_call(contract_kernel, grid=(slots, steps), out_shape=jax.ShapeD...]
    reshape x2 -> x0, local copies, waits for them, and re-layouts: 9.97 us -> none  [the longest x1 6.35 us: shards(): table = gathered.reshape(block_count, block_size, rank_width)]
  transfers between devices with their start and end apart: 3 -> 2, of which waited for: 3 -> 2; matrix products, arithmetic and copies ran while one was open for 4% -> 1% of each run, Pallas kernels for 0% -> 0%
where the time goes in v1:
time: 147 us; the launch traced here: 146 us
  blocking collectives  74.2 us (50%)
  Pallas kernels  32.9 us (22%)
  waiting for transfers between devices  19.3 us (13%)
  starting transfers between devices  12.8 us (9%)
  local copies, waits for them, and re-layouts  5.78 us (4%)
    all_to_all x1, blocking collectives, shards(): lax.all_to_all(total.reshape(owners, per_owner, width, BS), BLK, 0, 0, ti...  33.8 us
    pallas_call x1, Pallas kernels, shards(): pl.pallas_call(contract_kernel, grid=(slots, steps), out_shape=jax.ShapeD...  26 us
    all_to_all x1, blocking collectives, shards(): parts = lax.all_to_all(parts, 'rep', 0, 0, tiled=True)  20.2 us
    all_to_all x1, waiting for transfers between devices, shards(): chosen = lax.all_to_all(chosen, 'rep', 0, 0, tiled=True)  15.3 us
    all_gather x1, blocking collectives, shards(): names = lax.all_gather(triples.reshape(1, named), 'rep', axis=0, tiled=True)  11.3 us
    all_to_all x1, blocking collectives, gathered(): lax.all_to_all(jnp.broadcast_to(array[None], (peers, *array.shape)), axis...  8.88 us
    all_to_all x1, starting transfers between devices, gathered(): lax.all_to_all(jnp.broadcast_to(array[None], (peers, *array.shape)), axis...  8.47 us
    all_to_all x1, starting transfers between devices, shards(): chosen = lax.all_to_all(chosen, 'rep', 0, 0, tiled=True)  4.3 us
  transfers between devices with their start and end apart: 2, of which 2 were waited for; matrix products, arithmetic and copies ran while one was open for 1% of the time, Pallas kernels for 0%

profile of v1, /device:TPU:8, one launch (start us, length us, event | category | flops | bytes accessed | tf_op | source)
XLA Modules:
  0.0 145.6 jit_solution(2104230136896581624)
XLA Ops:
  0.0 0.0 copy-start
  0.0 0.7 copy-done
  0.7 0.0 copy-start.3
  0.7 8.9 %all_to_all.25 = bf16[4,2,32,128]{3,2,1,0:T(8,128)(2,1)S(1)} all-to-all(bf16[4,2,32,128]{3,2,1,0:T(8,128)(2,1)S(1)} %broadcast_in_dim.4), channel_id=1, replica_groups=mesh['blk_0'=8,'blk_1'=4,'rep'=8] {'blk_1'}, dimensions={0} | all-to-all | bytes 131072 | tf_op jit(solution)/shard_map/all_to_all | solution.py:151
  9.6 0.9 broadcast_in_dim.5
  10.5 8.5 %all-to-all-start.1 = ((bf16[8,4,2,32,128]{4,3,2,1,0:T(8,128)(2,1)}), bf16[8,4,2,32,128]{4,3,2,1,0:T(8,128)(2,1)S(1)}, u32[]{:S(2)}, u32[]{:S(2)}) async-start(bf16[8,4,2,32,128]{4,3,2,1,0:T(8,128)(2,1)} %broadcast_in_dim.5), calls=%async_computation.1 | async-start | bytes 1048576 | tf_op jit(solution)/shard_map/all_to_all | solution.py:151
  19.0 0.8 reshape.18
  19.8 11.3 %all-gather = s32[8,1,6]{2,1,0:T(1,128)} all-gather(s32[1,1,6]{2,1,0:T(1,128)S(1)} %reshape.18), channel_id=1, replica_groups=mesh['blk_0'=8,'blk_1'=4,'rep'=8] {'rep'}, dimensions={0}, use_global_device_ids=true | all-gather | bytes 216 | tf_op jit(solution)/shard_map/all_gather | solution.py:165
  31.1 4.0 %all-to-all-done.1 = bf16[8,4,2,32,128]{4,3,2,1,0:T(8,128)(2,1)S(1)} async-done(((bf16[8,4,2,32,128]{4,3,2,1,0:T(8,128)(2,1)}), bf16[8,4,2,32,128]{4,3,2,1,0:T(8,128)(2,1)S(1)}, u32[]{:S(2)}, u32[]{:S(2)}) %all-to-all-start.1) | async-done | bytes 524320 | tf_op jit(solution)/shard_map/all_to_all | solution.py:151
  35.1 0.0 copy-start.2
  35.1 0.0 copy-done.3
  35.1 0.8 copy-done.2
  35.9 2.1 %select.1 = bf16[8,16,32,128]{3,2,1,0:T(8,128)(2,1)} custom-call(s32[8,6]{1,0:T(8,128)} %bitcast.13, bf16[64,32,128]{2,1,0:T(8,128)(2,1)} %bitcast.11, bf16[2,32,128]{2,1,0:T(8,128)(2,1)} %copy-done.3), custom_call_target="tpu_custom_call" | custom-call | tf_op jit(solution)/shard_map/select/pallas_call | solution.py:170
  38.0 4.3 %all-to-all-start.2 = ((bf16[8,16,32,128]{3,2,1,0:T(8,128)(2,1)}), bf16[8,16,32,128]{3,2,1,0:T(8,128)(2,1)S(1)}, u32[]{:S(2)}, u32[]{:S(2)}) async-start(bf16[8,16,32,128]{3,2,1,0:T(8,128)(2,1)} %select.1), calls=%async_computation.2 | async-start | bytes 2097152 | tf_op jit(solution)/shard_map/all_to_all | solution.py:177
  42.9 15.3 %all-to-all-done.2.sel.own = bf16[8,16,32,128]{3,2,1,0:T(8,128)(2,1)S(1)} async-done(((bf16[8,16,32,128]{3,2,1,0:T(8,128)(2,1)}), bf16[8,16,32,128]{3,2,1,0:T(8,128)(2,1)S(1)}, u32[]{:S(2)}, u32[]{:S(2)}) %all-to-all-start.2) | async-done | bytes 1048608 | tf_op jit(solution)/shard_map/all_to_all | solution.py:177
  58.2 0.0 copy-start.1
  58.2 1.0 copy-done.1
  59.2 26.0 %contract.1 = f32[8,8,32,128]{3,2,1,0:T(8,128)} custom-call(s32[2,3]{1,0:T(2,128)} %triples.1, s32[1]{0:T(128)S(6)} %copy.12.count, bf16[2,128,128,128]{3,2,1,0:T(8,128)(2,1)} %x.1, bf16[8,16,32,128]{3,2,1,0:T(8,128)(2,1)} %copy-done.1), custom_call_target="tpu_custom_call" | custom-call | tf_op jit(solution)/shard_map/contract/pallas_call | solution.py:179
  85.1 20.2 %all_to_all.26.parts = f32[8,8,32,128]{3,2,1,0:T(8,128)} all-to-all(f32[8,8,32,128]{3,2,1,0:T(8,128)} %contract.1), channel_id=1, replica_groups=mesh['blk_0'=8,'blk_1'=4,'rep'=8] {'rep'}, dimensions={0} | all-to-all | bytes 2097152 | tf_op jit(solution)/shard_map/all_to_all | solution.py:200
  105.3 2.8 %scatter.1 = (f32[64,32,128]{2,1,0:T(8,128)}, f32[2,32,128]{2,1,0:T(8,128)}) custom-call(s32[8,6]{1,0:T(8,128)} %bitcast.14, f32[8,8,32,128]{3,2,1,0:T(8,128)} %all_to_all.26.parts, bf16[8,16,32,128]{3,2,1,0:T(8,128)(2,1)} %copy-done.1), custom_call_target="tpu_custom_call" | custom-call | tf_op jit(solution)/shard_map/scatter/pallas_call | solution.py:201
  108.2 33.8 %all_to_all.27.arrived = f32[32,2,32,128]{3,2,1,0:T(8,128)} all-to-all(f32[32,2,32,128]{3,2,1,0:T(8,128)} %bitcast.12), channel_id=1, replica_groups=mesh['blk_0'=8,'blk_1'=4,'rep'=8] {'blk_0','blk_1'}, dimensions={0} | all-to-all | bytes 2097152 | tf_op jit(solution)/shard_map/all_to_all | solution.py:211
  142.0 2.0 %finish.1 = f32[256,32]{1,0:T(8,128)} custom-call(f32[32,2,32,128]{3,2,1,0:T(8,128)} %all_to_all.27.arrived, f32[2,32,128]{2,1,0:T(8,128)} %get-tuple-element.8.fitted), custom_call_target="tpu_custom_call" | custom-call | tf_op jit(solution)/shard_map/finish/pallas_call | solution.py:214
  144.0 1.6 %copy.9 = f32[256,32]{0,1:T(8,128)} copy(f32[256,32]{1,0:T(8,128)} %finish.1) | data formatting | bytes 65536 | tf_op jit(solution)/shard_map/finish/pallas_call | solution.py:214
  (2 shorter events, 0.0 us)
Async XLA Ops:
  0.0 0.7 copy-start
  0.7 34.4 %copy-start.3 = (bf16[2,32,128]{2,1,0:T(8,128)(2,1)}, bf16[2,32,128]{2,1,0:T(8,128)(2,1)S(1)}, u32[]{:S(2)}) copy-start(bf16[2,32,128]{2,1,0:T(8,128)(2,1)S(1)} %bitcast_bitcast_fusion.own) | copy-start | bytes 49156
  10.5 24.5 %all-to-all-start.1 = ((bf16[8,4,2,32,128]{4,3,2,1,0:T(8,128)(2,1)}), bf16[8,4,2,32,128]{4,3,2,1,0:T(8,128)(2,1)S(1)}, u32[]{:S(2)}, u32[]{:S(2)}) async-start(bf16[8,4,2,32,128]{4,3,2,1,0:T(8,128)(2,1)} %broadcast_in_dim.5), calls=%async_computation.1 | async-start | bytes 1048576 | tf_op jit(solution)/shard_map/all_to_all | solution.py:151
  35.1 0.8 copy-start.2
  38.0 20.2 %all-to-all-start.2 = ((bf16[8,16,32,128]{3,2,1,0:T(8,128)(2,1)}), bf16[8,16,32,128]{3,2,1,0:T(8,128)(2,1)S(1)}, u32[]{:S(2)}, u32[]{:S(2)}) async-start(bf16[8,16,32,128]{3,2,1,0:T(8,128)(2,1)} %select.1), calls=%async_computation.2 | async-start | bytes 2097152 | tf_op jit(solution)/shard_map/all_to_all | solution.py:177
  58.2 1.0 copy-start.1
